TPU v7x, 128 devices: a whole 4x4x4 slice. The times are simulated.
128 devices in a mesh: row: 8 (over z_lo, y), col: 16 (over x, z_hi, core).
Axes of the slice: x: 4, y: 4, z: 4 (z_hi: 2, z_lo: 2; z = z_hi * 2 + z_lo), core: 2. Of those that a mesh axis runs over, the one named last changes fastest.
Arguments:
- panel: bfloat16 [524288, 256], P(('row', 'col')), may hold values from -6 to 6
- row_basis: bfloat16 [524288, 16], P('row'), may hold values from -1.5 to 1.5
- col_basis: bfloat16 [524288, 16], P(('row', 'col')), may hold values from -0.375 to 0.375
- near_blocks: bfloat16 [2048, 9, 256, 256], P(('row', 'col')), may hold values from -0.125 to 0.125
- couplings: bfloat16 [8, 16, 512, 16, 16], P('row', 'col'), may hold values from -0.375 to 0.375
- blk_rows: int32 [8, 16, 512], P('row', 'col'), may hold values from 0 to 255
- blk_cols: int32 [8, 16, 512], P('row', 'col'), may hold values from 0 to 127
- blk_count: int32 [8, 16], P('row', 'col'), may hold values from 64 to 512, as said below
Outputs:
- product: bfloat16 [524288, 256], P(('row', 'col'))
Inputs may be any that keep to these rules, and one draw needn't show every extreme that they name: `blk_count`: slots at or past a device's count hold in-range indices and are not part of the matrix; in every draw some device holds 512 live slots.
All inputs are finite; a program needn't handle non-finite values.
Results may differ from a plain program's by a relative error of at most 0.0052.
Values may be sent and summed in bfloat16 or wider, within the bound.
A program may use at most 192 MiB of HBM per device.

v0:
```python
import jax
import jax.numpy as jnp
from jax import lax
from jax.sharding import PartitionSpec as P


def padded_2(array, sides, width):
    edges = {}
    for axis, dim in sides:
        peers, length = (lax.axis_size(axis), array.shape[dim])
        up = [(i, (i + 1) % peers) for i in range(peers - 1)]
        last = lax.slice_in_dim(array, length - width, length, axis=dim)
        leading = lax.slice_in_dim(array, 0, width, axis=dim)
        edges[dim] = (
            lax.ppermute(last, axis, up),
            lax.ppermute(leading, axis, [(b, a) for a, b in up]),
        )
    done = []
    for _, dim in sides:
        low, high = edges[dim]
        around = [(width, width) if d in done else (0, 0) for d in range(array.ndim)]
        array = jnp.concatenate([jnp.pad(low, around), array, jnp.pad(high, around)], axis=dim)
        done.append(dim)
    return array


def laid_out(parts, dim):
    lengths = list(parts.shape[1:])
    lengths[dim] *= parts.shape[0]
    return jnp.moveaxis(parts, 0, dim).reshape(lengths)


def copy_for_each(array, axis):
    peers = lax.axis_size(axis)
    return lax.all_to_all(
        jnp.broadcast_to(array[None], (peers, *array.shape)), axis, 0, 0, tiled=True
    )


def gather_directly(array, axis, dim):
    return laid_out(copy_for_each(array, axis), dim)


def cut_along(array, dim, peers):
    before, after = (array.shape[:dim], array.shape[dim + 1 :])
    return jnp.moveaxis(array.reshape(*before, peers, -1, *after), dim, 0)


def sent_and_summed(array, axis, dim):
    parts = cut_along(array, dim, lax.axis_size(axis))
    arrived = lax.all_to_all(parts, axis, split_axis=0, concat_axis=0, tiled=True)
    return arrived.astype(jnp.float32).sum(axis=0)


def near_part(panel, near_blocks):
    own_rows, panel_cols = panel.shape
    leaf_size = near_blocks.shape[2]
    near_count = near_blocks.shape[1]
    half_band = near_count // 2
    cluster_dev = own_rows // leaf_size
    padded = padded_2(panel, ((("row", "col"), 0),), half_band * leaf_size)
    windows = padded.reshape(cluster_dev + 2 * half_band, leaf_size, panel_cols)
    stacked = jnp.stack(
        [windows[offset : offset + cluster_dev] for offset in range(near_count)], axis=1
    )
    result = jnp.einsum("kopq,koqn->kpn", near_blocks, stacked, preferred_element_type=jnp.float32)
    return result.reshape(own_rows, panel_cols)


def far_part(panel, row_basis, col_basis, couplings, blk_rows, blk_cols, blk_count, leaf_size):
    own_rows, panel_cols = panel.shape
    rank_size = col_basis.shape[1]
    cluster_dev = own_rows // leaf_size
    coeffs = jnp.einsum(
        "kpr,kpn->krn",
        col_basis.reshape(cluster_dev, leaf_size, rank_size),
        panel.reshape(cluster_dev, leaf_size, panel_cols),
        preferred_element_type=jnp.float32,
    ).astype(jnp.bfloat16)
    gathered = gather_directly(coeffs, "row", 0)
    slots = couplings.shape[2]
    picked = gathered[blk_cols.reshape(slots)]
    block_terms = jnp.einsum(
        "bij,bjn->bin",
        couplings.reshape(slots, rank_size, rank_size),
        picked,
        preferred_element_type=jnp.float32,
    )
    group_clusters = lax.axis_size("col") * cluster_dev
    is_live = jnp.arange(slots, dtype=jnp.int32) < blk_count.reshape(())
    one_hot = (
        (blk_rows.reshape(slots)[None, :] == jnp.arange(group_clusters, dtype=jnp.int32)[:, None])
        & is_live[None, :]
    ).astype(jnp.float32)
    partial_value = jnp.dot(
        one_hot, block_terms.reshape(slots, rank_size * panel_cols), precision=lax.Precision.HIGHEST
    )
    partial_value = partial_value.reshape(group_clusters, rank_size, panel_cols)
    coupled = sent_and_summed(partial_value.astype(jnp.bfloat16), "col", 0)
    own_basis = lax.dynamic_slice_in_dim(row_basis, lax.axis_index("col") * own_rows, own_rows, 0)
    own_basis = own_basis.reshape(cluster_dev, leaf_size, rank_size).astype(jnp.float32)
    return jnp.einsum("kpr,krn->kpn", own_basis, coupled, precision=lax.Precision.HIGHEST).reshape(
        own_rows, panel_cols
    )


def on_device(panel, row_basis, col_basis, near_blocks, couplings, blk_rows, blk_cols, blk_count):
    leaf_size = near_blocks.shape[2]
    far_field = far_part(
        panel, row_basis, col_basis, couplings, blk_rows, blk_cols, blk_count, leaf_size
    )
    near_field = near_part(panel, near_blocks)
    return (near_field + far_field).astype(jnp.bfloat16)


def solution(mesh):
    placed = (
        P(("row", "col"), None),
        P("row", None),
        P(("row", "col"), None),
        P(("row", "col"), None, None, None),
        P("row", "col", None, None, None),
        P("row", "col", None),
        P("row", "col", None),
        P("row", "col"),
    )
    return jax.shard_map(
        on_device, mesh=mesh, in_specs=placed, out_specs=P(("row", "col"), None), check_vma=False
    )
```

profile of v0, /device:TPU:16, one launch (start us, length us, event | category | flops | bytes accessed | tf_op | source)
XLA Modules:
  0.0 141.0 jit_solution(13548000087172162547)
XLA Ops:
  0.0 0.0 copy-start
  0.0 2.5 %fusion.14 = (bf16[1024,256]{1,0:T(8,128)(2,1)}, bf16[1024,256]{1,0:T(8,128)(2,1)}) fusion(bf16[4096,256]{1,0:T(8,128)(2,1)} %param.8), kind=kLoop, calls=%fused_computation.36 | loop fusion | bytes 2097152 | tf_op jit(solution)/shard_map/slice | solution.py:13
  2.5 1.9 %collective-permute-start = (bf16[1024,256]{1,0:T(8,128)(2,1)}, bf16[1024,256]{1,0:T(8,128)(2,1)S(1)}, u32[]{:S(2)}, u32[]{:S(2)}) collective-permute-start(bf16[1024,256]{1,0:T(8,128)(2,1)} %get-tuple-element.14), channel_id=1, source_target_pairs={{0,1},{1,2},{2,3},{3,4},{4,5},{5,6},{6,7},{7,8},{8,9},{9,10},{10,1... | collective-permute-start | bytes 1572872 | tf_op jit(solution)/shard_map/ppermute | solution.py:15
  4.4 8.2 %collective-permute-start.1 = (bf16[1024,256]{1,0:T(8,128)(2,1)}, bf16[1024,256]{1,0:T(8,128)(2,1)S(1)}, u32[]{:S(2)}, u32[]{:S(2)}) collective-permute-start(bf16[1024,256]{1,0:T(8,128)(2,1)} %get-tuple-element.13), channel_id=1, source_target_pairs={{1,0},{2,1},{3,2},{4,3},{5,4},{6,5},{7,6},{8,7},{9,8},{10,9},{11,1... | collective-permute-start | bytes 1572872 | tf_op jit(solution)/shard_map/ppermute | solution.py:16
  12.5 0.0 copy-start.4
  12.6 0.0 copy-start.2
  12.6 2.1 %convolution_convert_fusion.1 = bf16[16,16,256]{2,1,0:T(8,128)(2,1)S(1)} fusion(bf16[16,256,256]{2,1,0:T(8,128)(2,1)} %bitcast.53, bf16[2,16,8,256]{3,2,1,0:T(8,128)(2,1)} %bitcast.66), kind=kOutput, calls=%fused_computation.5 | convolution fusion | flops 33619968 | bytes 2359296 | tf_op jit(solution)/shard_map/kpr,kpn->krn/dot_general | solution.py:74
  14.7 1.1 broadcast_in_dim.2
  15.7 6.2 %all-to-all-start = ((bf16[8,16,16,256]{3,2,1,0:T(8,128)(2,1)}), bf16[8,16,16,256]{3,2,1,0:T(8,128)(2,1)}, u32[]{:S(2)}, u32[]{:S(2)}) async-start(bf16[8,16,16,256]{3,2,1,0:T(8,128)(2,1)} %broadcast_in_dim.2), calls=%async_computation | async-start | bytes 2097152 | tf_op jit(solution)/shard_map/all_to_all | solution.py:35
  21.9 0.0 copy-done.4
  21.9 0.0 copy-done.2
  21.9 2.8 %copy.17 = bf16[512,16,16]{2,1,0:T(8,128)(2,1)} copy(bf16[512,16,16]{0,2,1:T(8,128)(2,1)S(1)} %bitcast.65) | data formatting | bytes 524288 | tf_op jit(solution)/shard_map/reshape | solution.py:85
  25.4 0.0 copy-done
  25.4 0.0 collective-permute-done
  25.5 1.9 %constant_dynamic-update-slice_fusion.3 = (bf16[5120,256]{1,0:T(8,128)(2,1)S(1)}, bf16[5120,256]{1,0:T(8,128)(2,1)S(1)}) fusion(bf16[4096,256]{1,0:T(8,128)(2,1)} %param.8, bf16[5120,256]{1,0:T(8,128)(2,1)S(1)} %constant_dynamic-update-slice_fusion.1), kind=kLoop, calls=%fused_computation.20 | loop fusion | bytes 6291456
  27.3 0.6 fusion.13
  27.9 1.5 %constant_dynamic-update-slice_fusion.12 = bf16[16,9,256,256]{3,2,1,0:T(8,128)(2,1)} fusion(bf16[16,1,256,256]{3,2,1,0:T(8,128)(2,1)S(1)} %bitcast.63), kind=kLoop, calls=%fused_computation.29 | loop fusion | bytes 4194304
  29.5 1.5 %constant_dynamic-update-slice_fusion.11 = bf16[16,9,256,256]{3,2,1,0:T(8,128)(2,1)} fusion(bf16[16,9,256,256]{3,2,1,0:T(8,128)(2,1)} %constant_dynamic-update-slice_fusion.12, bf16[16,1,256,256]{3,2,1,0:T(8,128)(2,1)S(1)} %bitcast.61), kind=kLoop, calls=%fused_computation.28 | loop fusion | bytes 4194304
  31.0 1.5 %constant_dynamic-update-slice_fusion.10 = bf16[16,9,256,256]{3,2,1,0:T(8,128)(2,1)} fusion(bf16[16,9,256,256]{3,2,1,0:T(8,128)(2,1)} %constant_dynamic-update-slice_fusion.11, bf16[16,1,256,256]{3,2,1,0:T(8,128)(2,1)S(1)} %bitcast.59), kind=kLoop, calls=%fused_computation.27 | loop fusion | bytes 4194304
  32.5 1.6 %constant_dynamic-update-slice_fusion.9 = bf16[16,9,256,256]{3,2,1,0:T(8,128)(2,1)} fusion(bf16[16,9,256,256]{3,2,1,0:T(8,128)(2,1)} %constant_dynamic-update-slice_fusion.10, bf16[16,1,256,256]{3,2,1,0:T(8,128)(2,1)S(1)} %bitcast.57), kind=kLoop, calls=%fused_computation.26 | loop fusion | bytes 4194304
  34.1 0.0 all-to-all-done
  34.1 4.2 %gather_fusion = bf16[512,16,256]{2,1,0:T(8,128)(2,1)} fusion(bf16[128,16,256]{2,1,0:T(8,128)(2,1)} %bitcast.16, s32[1024]{0:T(1024)S(1)} %pad_clamp_fusion), kind=kCustom, calls=%fused_computation | custom fusion | bytes 8390656 | tf_op jit(solution)/shard_map/gather | solution.py:82
  38.3 4.0 %fusion.15 = f32[512,256,16]{1,2,0:T(8,128)S(1)} fusion(bf16[512,16,16]{2,1,0:T(8,128)(2,1)} %copy.17, bf16[512,16,256]{2,1,0:T(8,128)(2,1)} %gather_fusion), kind=kOutput, calls=%fused_computation.37 | convolution fusion | flops 67108864 | bytes 12845056 | tf_op jit(solution)/shard_map/bij,bjn->bin/dot_general | solution.py:83
  42.3 11.5 %copy.27 = f32[64,8,16,256]{3,1,2,0:T(8,128)} copy(f32[64,8,16,256]{3,2,1,0:T(8,128)S(1)} %bitcast.50) | data formatting | bytes 16777216
  53.8 0.0 copy-start.3
  53.8 9.0 %copy.18 = f32[4096,512]{1,0:T(8,128)} copy(f32[4096,512]{0,1:T(8,128)} %bitcast.52) | data formatting | bytes 16777216 | tf_op jit(solution)/shard_map/dot_general | solution.py:95
  62.9 0.0 copy-done.3
  62.9 12.9 %convolution_convert_fusion = bf16[256,16,256]{2,0,1:T(8,128)(2,1)S(1)} fusion(f32[16,256,512]{2,1,0:T(8,128)} %bitcast.51, s32[512]{0:T(512)S(1)} %bitcast.68, pred[512]{0:T(512)(128)(4,1)S(1)} %iota_compare_fusion.1), kind=kOutput, calls=%fused_computation.4 | convolution fusion | flops 6443761664 | bytes 10488320 | tf_op jit(solution)/shard_map/dot_general | solution.py:95
  75.8 1.5 %copy.19 = bf16[16,16,16,256]{3,1,2,0:T(8,128)(2,1)} copy(bf16[16,16,16,256]{3,1,0,2:T(8,128)(2,1)S(1)} %bitcast.55) | data formatting | bytes 4194304 | tf_op jit(solution)/shard_map/reshape | solution.py:46
  77.3 12.0 %all-to-all-start.1 = ((bf16[16,16,16,256]{3,1,2,0:T(8,128)(2,1)}), bf16[16,16,16,256]{3,1,2,0:T(8,128)(2,1)}, u32[]{:S(2)}, u32[]{:S(2)}) async-start(bf16[16,16,16,256]{3,1,2,0:T(8,128)(2,1)} %copy.19), calls=%async_computation.1 | async-start | bytes 4194304 | tf_op jit(solution)/shard_map/all_to_all | solution.py:51
  89.3 3.1 %constant_dynamic-update-slice_fusion.8 = bf16[16,9,256,256]{3,2,1,0:T(8,128)(2,1)} fusion(bf16[16,9,256,256]{3,2,1,0:T(8,128)(2,1)} %constant_dynamic-update-slice_fusion.9, bf16[16,1,256,256]{3,2,1,0:T(8,128)(2,1)} %bitcast.54), kind=kLoop, calls=%fused_computation.25 | loop fusion | bytes 4194304
  92.4 0.0 collective-permute-done.1
  92.4 0.6 fusion.12
  93.1 1.5 %constant_dynamic-update-slice_fusion.7 = bf16[16,9,256,256]{3,2,1,0:T(8,128)(2,1)} fusion(bf16[16,9,256,256]{3,2,1,0:T(8,128)(2,1)} %constant_dynamic-update-slice_fusion.8, bf16[16,1,256,256]{3,2,1,0:T(8,128)(2,1)S(1)} %bitcast.62), kind=kLoop, calls=%fused_computation.24 | loop fusion | bytes 4194304
  94.6 1.5 %constant_dynamic-update-slice_fusion.6 = bf16[16,9,256,256]{3,2,1,0:T(8,128)(2,1)} fusion(bf16[16,9,256,256]{3,2,1,0:T(8,128)(2,1)} %constant_dynamic-update-slice_fusion.7, bf16[16,1,256,256]{3,2,1,0:T(8,128)(2,1)S(1)} %bitcast.60), kind=kLoop, calls=%fused_computation.23 | loop fusion | bytes 4194304
  96.1 1.5 %constant_dynamic-update-slice_fusion.5 = bf16[16,9,256,256]{3,2,1,0:T(8,128)(2,1)} fusion(bf16[16,9,256,256]{3,2,1,0:T(8,128)(2,1)} %constant_dynamic-update-slice_fusion.6, bf16[16,1,256,256]{3,2,1,0:T(8,128)(2,1)S(1)} %bitcast.58), kind=kLoop, calls=%fused_computation.22 | loop fusion | bytes 4194304
  97.7 1.5 %constant_dynamic-update-slice_fusion.4 = bf16[16,9,256,256]{3,2,1,0:T(8,128)(2,1)} fusion(bf16[16,9,256,256]{3,2,1,0:T(8,128)(2,1)} %constant_dynamic-update-slice_fusion.5, bf16[16,1,256,256]{3,2,1,0:T(8,128)(2,1)S(1)} %bitcast.56), kind=kLoop, calls=%fused_computation.21 | loop fusion | bytes 4194304 | tf_op jit(solution)/shard_map/stack | solution.py:63
  99.2 19.3 %all-to-all-done.1 = bf16[16,16,16,256]{3,1,2,0:T(8,128)(2,1)} async-done(((bf16[16,16,16,256]{3,1,2,0:T(8,128)(2,1)}), bf16[16,16,16,256]{3,1,2,0:T(8,128)(2,1)}, u32[]{:S(2)}, u32[]{:S(2)}) %all-to-all-start.1) | async-done | bytes 2097184 | tf_op jit(solution)/shard_map/all_to_all | solution.py:51
  118.5 1.9 %convert_reduce_fusion = f32[16,16,256]{2,0,1:T(8,128)S(1)} fusion(bf16[16,16,16,256]{3,1,2,0:T(8,128)(2,1)} %all-to-all-done.1), kind=kLoop, calls=%fused_computation.3 | loop fusion | flops 2031616 | bytes 2359296 | tf_op jit(solution)/shard_map/reduce_sum | solution.py:52
  120.4 3.9 %fusion.4 = f32[16,256,256]{2,1,0:T(8,128)} fusion(f32[16,16,256]{2,0,1:T(8,128)S(1)} %convert_reduce_fusion, bf16[2,16,8,256]{3,2,1,0:T(8,128)(2,1)S(1)} %bitcast.64), kind=kOutput, calls=%fused_computation.9 | convolution fusion | flops 201326592 | bytes 4587520 | tf_op jit(solution)/shard_map/kpr,krn->kpn/dot_general | solution.py:102
  124.3 0.0 copy-start.1
  124.3 16.7 %fusion = bf16[16,256,256]{2,1,0:T(8,128)(2,1)} fusion(f32[16,256,256]{2,1,0:T(8,128)} %fusion.4, bf16[16,9,256,256]{3,2,1,0:T(8,128)(2,1)} %param.11, bf16[16,9,256,256]{3,2,1,0:T(8,128)(2,1)} %constant_dynamic-update-slice_fusion.4), kind=kOutput, calls=%fused_computation.2 | convolution fusion | flops 4833935360 | bytes 44040192 | tf_op jit(solution)/shard_map/kopq,koqn->kpn/dot_general | solution.py:66
  141.0 0.0 copy-done.1
  (6 shorter events, 0.1 us)
Async XLA Ops:
  0.0 25.4 %copy-start = (bf16[65536,16]{0,1:T(8,128)(2,1)S(1)}, bf16[65536,16]{0,1:T(8,128)(2,1)}, u32[]{:S(2)}) copy-start(bf16[65536,16]{0,1:T(8,128)(2,1)} %param.9) | copy-start | bytes 6291460
  2.5 22.9 %collective-permute-start = (bf16[1024,256]{1,0:T(8,128)(2,1)}, bf16[1024,256]{1,0:T(8,128)(2,1)S(1)}, u32[]{:S(2)}, u32[]{:S(2)}) collective-permute-start(bf16[1024,256]{1,0:T(8,128)(2,1)} %get-tuple-element.14), channel_id=1, source_target_pairs={{0,1},{1,2},{2,3},{3,4},{4,5},{5,6},{6,7},{7,8},{8,9},{9,10},{10,1... | collective-permute-start | bytes 1572872 | tf_op jit(solution)/shard_map/ppermute | solution.py:15
  4.4 88.0 %collective-permute-start.1 = (bf16[1024,256]{1,0:T(8,128)(2,1)}, bf16[1024,256]{1,0:T(8,128)(2,1)S(1)}, u32[]{:S(2)}, u32[]{:S(2)}) collective-permute-start(bf16[1024,256]{1,0:T(8,128)(2,1)} %get-tuple-element.13), channel_id=1, source_target_pairs={{1,0},{2,1},{3,2},{4,3},{5,4},{6,5},{7,6},{8,7},{9,8},{10,9},{11,1... | collective-permute-start | bytes 1572872 | tf_op jit(solution)/shard_map/ppermute | solution.py:16
  12.5 9.4 %copy-start.4 = (s32[1,1,512]{2,1,0:T(1,128)S(1)}, s32[1,1,512]{2,1,0:T(1,128)}, u32[]{:S(2)}) copy-start(s32[1,1,512]{2,1,0:T(1,128)} %param.14) | copy-start | bytes 6148
  12.6 9.4 %copy-start.2 = (bf16[1,1,512,16,16]{2,4,3,1,0:T(8,128)(2,1)S(1)}, bf16[1,1,512,16,16]{2,4,3,1,0:T(8,128)(2,1)}, u32[]{:S(2)}) copy-start(bf16[1,1,512,16,16]{2,4,3,1,0:T(8,128)(2,1)} %param.12) | copy-start | bytes 786436
  15.7 18.3 %all-to-all-start = ((bf16[8,16,16,256]{3,2,1,0:T(8,128)(2,1)}), bf16[8,16,16,256]{3,2,1,0:T(8,128)(2,1)}, u32[]{:S(2)}, u32[]{:S(2)}) async-start(bf16[8,16,16,256]{3,2,1,0:T(8,128)(2,1)} %broadcast_in_dim.2), calls=%async_computation | async-start | bytes 2097152 | tf_op jit(solution)/shard_map/all_to_all | solution.py:35
  53.8 9.1 %copy-start.3 = (s32[1,1,512]{2,1,0:T(1,128)S(1)}, s32[1,1,512]{2,1,0:T(1,128)}, u32[]{:S(2)}) copy-start(s32[1,1,512]{2,1,0:T(1,128)} %param.13) | copy-start | bytes 6148
  77.3 41.2 %all-to-all-start.1 = ((bf16[16,16,16,256]{3,1,2,0:T(8,128)(2,1)}), bf16[16,16,16,256]{3,1,2,0:T(8,128)(2,1)}, u32[]{:S(2)}, u32[]{:S(2)}) async-start(bf16[16,16,16,256]{3,1,2,0:T(8,128)(2,1)} %copy.19), calls=%async_computation.1 | async-start | bytes 4194304 | tf_op jit(solution)/shard_map/all_to_all | solution.py:51
  124.3 16.7 %copy-start.1 = (bf16[65536,16]{0,1:T(8,128)(2,1)S(1)}, bf16[65536,16]{0,1:T(8,128)(2,1)}, u32[]{:S(2)}) copy-start(bf16[65536,16]{0,1:T(8,128)(2,1)} %param.9) | copy-start | bytes 6291460
where the time goes:
time: 142 us; the launch traced here: 141 us
  local copies, waits for them, and re-layouts  51.1 us (36%)
  matrix products  39.6 us (28%)
  starting transfers between devices  28.2 us (20%)
  waiting for transfers between devices  19.3 us (14%)
  other arithmetic  1.92 us (1%)
    unnamed x21, local copies, waits for them, and re-layouts  27.3 us
    all_to_all x1, waiting for transfers between devices, sent_and_summed(): lax.all_to_all(parts, axis, split_axis=0, concat_axis=0, tiled=True)  19.3 us
    dot_general x1, matrix products, near_part(): jnp.einsum('kopq,koqn->kpn', near_blocks, stacked, preferred_element_type...  16.7 us
    dot_general x1, matrix products, far_part(): jnp.dot(one_hot, block_terms.reshape(slots, rank_size * panel_cols), prec...  12.9 us
    all_to_all x1, starting transfers between devices, sent_and_summed(): lax.all_to_all(parts, axis, split_axis=0, concat_axis=0, tiled=True)  12 us
    dot_general x1, local copies, waits for them, and re-layouts, far_part(): jnp.dot(one_hot, block_terms.reshape(slots, rank_size * panel_cols), prec...  9.05 us
    ppermute x1, starting transfers between devices, padded_2(): lax.ppermute(leading, axis, [(b, a) for a, b in up])  8.15 us
    all_to_all x1, starting transfers between devices, copy_for_each(): lax.all_to_all(jnp.broadcast_to(array[None], (peers, *array.shape)), axis...  6.16 us
  transfers between devices with their start and end apart: 4, of which 1 were waited for; matrix products, arithmetic and copies ran while one was open for 48% of the time, Pallas kernels for 0%

commit v1 on v0

v1 whole, which is shorter than its diff:
```python
import functools

import jax
import jax.numpy as jnp
from jax import lax
from jax.experimental import pallas as pl
from jax.experimental.pallas import tpu as pltpu
from jax.sharding import PartitionSpec as P

MESH = pl.DeviceIdType.MESH
F32 = jnp.float32
BF16 = jnp.bfloat16

LEAF = 256
R = 16
N = 256
K = 16
HALF = 4
NEAR = 9
SLOTS = 512
GROUPS = SLOTS // 16
ROWCL = 256


def mm(a, b):
    return jnp.dot(a, b, preferred_element_type=F32)


def mm_t(a, b):
    return lax.dot_general(a, b, (((0,), (0,)), ((), ())), preferred_element_type=F32)


def iota(shape, dim):
    return lax.broadcasted_iota(jnp.int32, shape, dim)


def kernel(
    panel_hbm, ut_hbm, vt_hbm, near_hbm, ct_hbm, rows_ref, cols_ref, cnt_ref,
    out_hbm,
    pext, vt, ut, ct, nb, nat, call, expand, lmat, xmat, tmat, ohc, ohr, uexp,
    pp, po, r0, qs, r1, r2, zs, r3, cpl, nearv, outv,
    lsem, nsem, osem, ssem, rsem,
):
    row = lax.axis_index("row")
    col = lax.axis_index("col")
    zl, y = row // 4, row % 4
    x, zh, core = col // 4, (col // 2) % 2, col % 2

    def at(zl_, y_, x_, zh_, core_):
        return (zl_ * 4 + y_, x_ * 4 + zh_ * 2 + core_)

    yp, ym = (y + 1) % 4, (y + 3) % 4
    xp, xm = (x + 1) % 4, (x + 3) % 4
    d_core = at(zl, y, x, zh, 1 - core)
    d_xp, d_xm = at(zl, y, xp, zh, core), at(zl, y, xm, zh, core)
    d_yp, d_ym = at(zl, yp, x, zh, core), at(zl, ym, x, zh, core)
    d_zl = at(1 - zl, y, x, zh, core)
    d_zh = at(zl, y, x, 1 - zh, core)
    lin = row * 16 + col
    has_l, has_r = lin > 0, lin < 127
    left, right = jnp.maximum(lin - 1, 0), jnp.minimum(lin + 1, 127)
    d_left, d_right = (left // 16, left % 16), (right // 16, right % 16)

    own = pl.ds(HALF * LEAF, K * LEAF)
    c_panel = pltpu.make_async_copy(panel_hbm, pext.at[own], lsem.at[0])
    c_vt = pltpu.make_async_copy(vt_hbm, vt, lsem.at[1])
    c_ct = pltpu.make_async_copy(ct_hbm, ct, lsem.at[2])
    c_ut = pltpu.make_async_copy(
        ut_hbm.at[:, pl.ds(pl.multiple_of(col * (K * LEAF), K * LEAF), K * LEAF)], ut, lsem.at[3]
    )
    c_panel.start()
    c_vt.start()

    barrier = pltpu.get_barrier_semaphore()
    for dev in (d_core, d_xp, d_xm, d_yp, d_ym, d_zl, d_zh):
        pl.semaphore_signal(barrier, inc=1, device_id=dev, device_id_type=MESH)

    @pl.when(has_l)
    def _():
        pl.semaphore_signal(barrier, inc=1, device_id=d_left, device_id_type=MESH)

    @pl.when(has_r)
    def _():
        pl.semaphore_signal(barrier, inc=1, device_id=d_right, device_id_type=MESH)

    c_ct.start()
    c_ut.start()

    def near_copy(k):
        return pltpu.make_async_copy(near_hbm.at[k], nb.at[k], nsem.at[k])

    near_order = list(range(4, 12)) + [3, 2, 1, 0] + list(range(12, 16))
    for k in near_order:
        near_copy(k).start()

    a256, b256 = iota((256, 256), 0), iota((256, 256), 1)
    perm = jnp.where((b256 // 16 == a256 % 16) & (b256 % 16 == a256 // 16), 1.0, 0.0).astype(BF16)
    e_mat = jnp.where(iota((R, 256), 1) // 16 == iota((R, 256), 0), 1.0, 0.0).astype(BF16)
    expand[...] = e_mat
    c_panel.wait()
    c_vt.wait()
    for k in range(K):
        nat[k * R:(k + 1) * R, :] = mm(
            vt[:, k * LEAF:(k + 1) * LEAF], pext[(HALF + k) * LEAF:(HALF + k + 1) * LEAF, :]
        ).astype(BF16)
    call[row] = mm(perm, nat[...]).astype(BF16).reshape(R, K, N)

    pl.semaphore_wait(barrier, 7 + has_l.astype(jnp.int32) + has_r.astype(jnp.int32))

    def rc(m, src, dst, dev):
        return pltpu.make_async_remote_copy(
            src_ref=src, dst_ref=dst, send_sem=ssem.at[m], recv_sem=rsem.at[m],
            device_id=dev, device_id_type=MESH,
        )

    def piece(m, slot, half, dev):
        ref = call.at[slot, pl.ds(half * 8, 8)]
        return rc(m, ref, ref, dev)

    s_zp = (1 - zl) * 4 + y
    s_ym, s_yp = zl * 4 + ym, zl * 4 + yp
    sz_ym, sz_yp = (1 - zl) * 4 + ym, (1 - zl) * 4 + yp
    ga = {
        0: piece(0, row, 0, d_zl), 1: piece(1, row, 1, d_zl),
        2: piece(2, row, 0, d_yp), 3: piece(3, row, 1, d_yp),
        4: piece(4, row, 0, d_ym), 5: piece(5, row, 1, d_ym),
        6: piece(6, s_zp, 0, d_yp), 7: piece(7, s_zp, 1, d_yp),
        8: piece(8, s_zp, 0, d_ym), 9: piece(9, s_zp, 1, d_ym),
        10: piece(10, s_ym, 0, d_yp), 11: piece(11, s_yp, 1, d_ym),
        12: piece(12, sz_ym, 0, d_yp), 13: piece(13, sz_yp, 1, d_ym),
    }
    for m in (0, 1, 2, 5, 3, 4):
        ga[m].start()

    tail = pl.ds(K * LEAF, HALF * LEAF)
    head = pl.ds(HALF * LEAF, HALF * LEAF)
    lo = pl.ds(0, HALF * LEAF)
    hi = pl.ds((HALF + K) * LEAF, HALF * LEAF)
    h_right = rc(30, pext.at[tail], pext.at[lo], d_right)
    h_left = rc(31, pext.at[head], pext.at[hi], d_left)

    @pl.when(has_r)
    def _():
        h_right.start()

    @pl.when(has_l)
    def _():
        h_left.start()

    c_ct.wait()

    def l_body(i, carry):
        v = mm_t(ct[i], expand[...])
        keep = iota((SLOTS, 256), 0) % 16 == iota((SLOTS, 256), 1) % 16
        lmat[:, i] = jnp.where(keep, v, 0.0).astype(BF16).reshape(GROUPS, 16, 256)
        return carry

    lax.fori_loop(0, R, l_body, 0)

    ga[2].wait_recv()
    ga[10].start()
    ga[5].wait_recv()
    ga[11].start()

    c_ut.wait()

    def u_body(k, carry):
        cols = pl.ds(pl.multiple_of(k * LEAF, LEAF), LEAF)
        v = mm_t(ut[:, cols], expand[...])
        keep = iota((LEAF, 256), 1) % 16 == k
        uexp[pl.ds(pl.multiple_of(k * LEAF, LEAF), LEAF), :] = jnp.where(keep, v, 0.0).astype(BF16)
        return carry

    lax.fori_loop(0, K, u_body, 0)

    ga[0].wait_recv()
    ga[6].start()
    ga[8].start()
    ga[1].wait_recv()
    ga[9].start()
    ga[7].start()

    oct_ = jnp.where(iota((128, SLOTS), 0) == cols_ref[...], 1.0, 0.0).astype(F32)
    ohc[...] = oct_.T.astype(BF16)
    ra = iota((ROWCL, SLOTS), 0)
    kk, dz, pos, dc = ra % 16, 1 - (ra // 16) % 2, (ra // 32) % 4, 1 - ra // 128
    dx = jnp.where(pos == 0, 2, jnp.where(pos == 1, 1, jnp.where(pos == 2, 3, 0)))
    cluster = (((x + dx) % 4) * 4 + ((zh + dz) % 2) * 2 + (core + dc) % 2) * 16 + kk
    live = iota((ROWCL, SLOTS), 1) < cnt_ref[0, 0]
    ohr[...] = jnp.where((cluster == rows_ref[...]) & live, 1.0, 0.0).astype(BF16)

    def near_row(k):
        acc = mm(nb[k, 0], pext[pl.ds(pl.multiple_of(k * LEAF, LEAF), LEAF), :])
        for o in range(1, NEAR):
            acc += mm(nb[k, o], pext[pl.ds(pl.multiple_of((k + o) * LEAF, LEAF), LEAF), :])
        nearv[k] = acc

    def near_rows(start, stop):
        def body(k, carry):
            near_copy(k).wait()
            near_row(k)
            return carry
        lax.fori_loop(start, stop, body, 0)

    near_rows(4, 8)
    ga[6].wait_recv()
    ga[12].start()
    ga[9].wait_recv()
    ga[13].start()
    near_rows(8, 12)
    for m in (3, 4, 10, 11, 7, 8, 12, 13):
        ga[m].wait_recv()

    def x_body(j, carry):
        cj = call[:, j].reshape(128, N)
        xmat[:, j] = mm(ohc[...], cj).astype(BF16).reshape(GROUPS, 16, N)
        return carry

    lax.fori_loop(0, R, x_body, 0)

    def t_body(g, carry):
        t = mm(lmat[g].reshape(256, 256), xmat[g].reshape(256, N))
        tmat[:, g] = t.astype(BF16).reshape(R, 16, N)
        return carry

    lax.fori_loop(0, GROUPS, t_body, 0)

    core_send = [rc(14 + h, pp.at[h], r0.at[h], d_core) for h in range(2)]
    for h in range(2):
        def p_body(i, carry, h=h):
            p = mm(ohr[...], tmat[h * 8 + i].reshape(SLOTS, N))
            pp[h, :, :, i] = p[:128].astype(BF16).reshape(4, 2, 16, N)
            po[h, :, :, i] = p[128:].reshape(4, 2, 16, N)
            return carry

        lax.fori_loop(0, 8, p_body, 0)
        core_send[h].start()

    b1p = [rc(16 + h, qs.at[h, 0, 0], r1.at[h, 0], d_xp) for h in range(2)]
    b1m = [rc(18 + h, qs.at[h, 0, 1], r1.at[h, 1], d_xm) for h in range(2)]
    b2p0 = [rc(20 + h, qs.at[h, 1, 1], r2.at[h, 0, 1], d_xp) for h in range(2)]
    b2m1 = [rc(22 + h, qs.at[h, 2, 0], r2.at[h, 1, 0], d_xm) for h in range(2)]
    b2p1 = [rc(24 + h, qs.at[h, 1, 0], r2.at[h, 0, 0], d_xp) for h in range(2)]
    b2m0 = [rc(26 + h, qs.at[h, 2, 1], r2.at[h, 1, 1], d_xm) for h in range(2)]
    bz = [rc(28 + h, zs.at[h], r3.at[h], d_zh) for h in range(2)]

    def fold(h, pos, dzi):
        return po[h, pos, dzi] + r0[h, pos, dzi].astype(F32)

    for h in range(2):
        core_send[h].wait_recv()
        qs[h, 0, 0] = fold(h, 0, 0).astype(BF16)
        qs[h, 0, 1] = fold(h, 0, 1).astype(BF16)
        b1p[h].start()
        b1m[h].start()
        qs[h, 1, 1] = fold(h, 1, 1).astype(BF16)
        qs[h, 2, 0] = fold(h, 2, 0).astype(BF16)
        b2p0[h].start()
        b2m1[h].start()

    @pl.when(has_l)
    def _():
        h_right.wait_recv()

    @pl.when(jnp.logical_not(has_l))
    def _():
        pext[lo] = jnp.zeros((HALF * LEAF, N), BF16)

    near_rows(0, 2)
    for h in range(2):
        b1p[h].wait_recv()
        qs[h, 1, 0] = (fold(h, 1, 0) + r1[h, 0].astype(F32)).astype(BF16)
        b2p1[h].start()
        b1m[h].wait_recv()
        qs[h, 2, 1] = (fold(h, 2, 1) + r1[h, 1].astype(F32)).astype(BF16)
        b2m0[h].start()

    near_rows(2, 4)

    @pl.when(has_r)
    def _():
        h_left.wait_recv()

    @pl.when(jnp.logical_not(has_r))
    def _():
        pext[hi] = jnp.zeros((HALF * LEAF, N), BF16)

    near_rows(12, 16)

    for h in range(2):
        b2p1[h].wait_recv()
        b2m1[h].wait_recv()
        zs[h] = (fold(h, 3, 0) + r2[h, 0, 0].astype(F32) + r2[h, 1, 0].astype(F32)).astype(BF16)
        bz[h].start()
    for h in range(2):
        b2p0[h].wait_recv()
        b2m0[h].wait_recv()
        po[h, 3, 1] = fold(h, 3, 1) + r2[h, 0, 1].astype(F32) + r2[h, 1, 1].astype(F32)
    for h in range(2):
        bz[h].wait_recv()
        cpl[pl.ds(h * 8, 8)] = (po[h, 3, 1] + r3[h].astype(F32)).astype(BF16)

    def out_copy(k):
        return pltpu.make_async_copy(
            outv.at[k], out_hbm.at[pl.ds(pl.multiple_of(k * LEAF, LEAF), LEAF)], osem.at[k]
        )

    def o_body(k, carry):
        far = mm(uexp[pl.ds(pl.multiple_of(k * LEAF, LEAF), LEAF), :], cpl[...].reshape(256, N))
        outv[k] = (nearv[k] + far).astype(BF16)
        out_copy(k).start()
        return carry

    lax.fori_loop(0, K, o_body, 0)

    for m in range(14):
        ga[m].wait_send()
    for group in (core_send, b1p, b1m, b2p0, b2m1, b2p1, b2m0, bz):
        for copy in group:
            copy.wait_send()

    @pl.when(has_r)
    def _():
        h_right.wait_send()

    @pl.when(has_l)
    def _():
        h_left.wait_send()

    def w_body(k, carry):
        out_copy(k).wait()
        return carry

    lax.fori_loop(0, K, w_body, 0)


def on_device(panel, row_basis, col_basis, near_blocks, couplings, blk_rows, blk_cols, blk_count):
    any_ = pl.BlockSpec(memory_space=pl.ANY)
    vm = pl.BlockSpec(memory_space=pltpu.VMEM)
    sm = pl.BlockSpec(memory_space=pltpu.SMEM)
    scratch = [
        pltpu.VMEM(((K + 2 * HALF) * LEAF, N), BF16),
        pltpu.VMEM((R, K * LEAF), BF16),
        pltpu.VMEM((R, K * LEAF), BF16),
        pltpu.VMEM((R, R, SLOTS), BF16),
        pltpu.VMEM((K, NEAR, LEAF, LEAF), BF16),
        pltpu.VMEM((K * R, N), BF16),
        pltpu.VMEM((8, R, K, N), BF16),
        pltpu.VMEM((R, 256), BF16),
        pltpu.VMEM((GROUPS, R, 16, 256), BF16),
        pltpu.VMEM((GROUPS, R, 16, N), BF16),
        pltpu.VMEM((R, GROUPS, 16, N), BF16),
        pltpu.VMEM((SLOTS, 128), BF16),
        pltpu.VMEM((ROWCL, SLOTS), BF16),
        pltpu.VMEM((K * LEAF, 256), BF16),
        pltpu.VMEM((2, 4, 2, 8, 16, N), BF16),
        pltpu.VMEM((2, 4, 2, 8, 16, N), F32),
        pltpu.VMEM((2, 4, 2, 8, 16, N), BF16),
        pltpu.VMEM((2, 3, 2, 8, 16, N), BF16),
        pltpu.VMEM((2, 2, 8, 16, N), BF16),
        pltpu.VMEM((2, 2, 2, 8, 16, N), BF16),
        pltpu.VMEM((2, 8, 16, N), BF16),
        pltpu.VMEM((2, 8, 16, N), BF16),
        pltpu.VMEM((R, K, N), BF16),
        pltpu.VMEM((K, LEAF, N), F32),
        pltpu.VMEM((K, LEAF, N), BF16),
        pltpu.SemaphoreType.DMA((4,)),
        pltpu.SemaphoreType.DMA((K,)),
        pltpu.SemaphoreType.DMA((K,)),
        pltpu.SemaphoreType.DMA((32,)),
        pltpu.SemaphoreType.DMA((32,)),
    ]
    return pl.pallas_call(
        kernel,
        out_shape=jax.ShapeDtypeStruct((K * LEAF, N), BF16),
        in_specs=[any_, any_, any_, any_, any_, vm, vm, sm],
        out_specs=any_,
        scratch_shapes=scratch,
        compiler_params=pltpu.CompilerParams(
            collective_id=0, has_side_effects=True, vmem_limit_bytes=66_000_000
        ),
    )(
        panel,
        row_basis.T,
        col_basis.T,
        near_blocks,
        couplings.reshape(SLOTS, R, R).transpose(1, 2, 0),
        blk_rows.reshape(1, SLOTS),
        blk_cols.reshape(1, SLOTS),
        blk_count,
    )


def solution(mesh):
    placed = (
        P(("row", "col"), None),
        P("row", None),
        P(("row", "col"), None),
        P(("row", "col"), None, None, None),
        P("row", "col", None, None, None),
        P("row", "col", None),
        P("row", "col", None),
        P("row", "col"),
    )
    return jax.shard_map(
        on_device, mesh=mesh, in_specs=placed, out_specs=P(("row", "col"), None), check_vma=False
    )
```

time: 142 us -> 64.6 us (0.45)
  the two profiles are of different devices: /device:TPU:16 before, /device:TPU:0 now
where the time goes in v1:
time: 64.6 us; the launch traced here: 64.4 us
  Pallas kernels  60.7 us (94%)
  local copies, waits for them, and re-layouts  3.05 us (5%)
  between operations  0.66 us (1%)
    pallas_call x1, Pallas kernels, on_device(): pl.pallas_call(kernel, out_shape=jax.ShapeDtypeStruct((K * LEAF, N), BF16...  60.7 us
    unnamed x1, local copies, waits for them, and re-layouts  3.05 us

profile of v1, /device:TPU:0, one launch (start us, length us, event | category | flops | bytes accessed | tf_op | source)
XLA Modules:
  0.0 64.4 jit_solution(15139623067185041976)
XLA Ops:
  0.7 60.7 %shard_map.82 = bf16[4096,256]{1,0:T(8,128)(2,1)} custom-call(bf16[4096,256]{1,0:T(8,128)(2,1)} %panel_hbm.1, bf16[16,65536]{1,0:T(8,128)(2,1)} %bitcast.7, bf16[16,4096]{1,0:T(8,128)(2,1)} %bitcast.9, bf16[16,9,256,256]{3,2,1,0:T(8,128)(2,1)} %near_hbm.1, bf16[16,16,512]{2,1,0:T(8,128)(2,1)} %bitcast.8, s32[1,512]{1,0:T(1,128)} %bitcast.10, ...), custom_call_target="tpu_custom_call" | custom-call | tf_op jit(solution)/shard_map/pallas_call | solution.py:373
  61.4 3.0 %copy.11 = bf16[4096,256]{1,0:T(8,128)(2,1)} copy(bf16[4096,256]{1,0:T(8,128)(2,1)} %shard_map.82) | data formatting | bytes 4194304

commit v2 on v1

v2 whole, which is shorter than its diff:
```python
import jax
import jax.numpy as jnp
from jax import lax
from jax.experimental import pallas as pl
from jax.experimental.pallas import tpu as pltpu
from jax.sharding import PartitionSpec as P

MESH = pl.DeviceIdType.MESH
F32 = jnp.float32
BF16 = jnp.bfloat16

LEAF = 256
R = 16
N = 256
HN = N // 2
K = 16
HALF = 4
NEAR = 9
SLOTS = 512
GROUPS = SLOTS // 16
ROWCL = 256


def mm(a, b):
    return jnp.dot(a, b, preferred_element_type=F32)


def mm_t(a, b):
    return lax.dot_general(a, b, (((0,), (0,)), ((), ())), preferred_element_type=F32)


def iota(shape, dim):
    return lax.broadcasted_iota(jnp.int32, shape, dim)


def kernel(
    panel_hbm, ut_hbm, vt_hbm, near_hbm, ct_hbm, rows_ref, cols_ref, cnt_ref,
    out_ref,
    pext, vt, ut, utt, ct, nb, call0, call1, expand, perm, lmat, tmat, ohr,
    pp, po, r0, qs, r1, r2, zs, r3, cplk, nearv,
    lsem, nsem, ssem, rsem,
):
    row = lax.axis_index("row")
    col = lax.axis_index("col")
    zl, y = row // 4, row % 4
    x, zh, core = col // 4, (col // 2) % 2, col % 2

    def at(zl_, y_, x_, zh_, core_):
        return (zl_ * 4 + y_, x_ * 4 + zh_ * 2 + core_)

    yp, ym = (y + 1) % 4, (y + 3) % 4
    xp, xm = (x + 1) % 4, (x + 3) % 4
    d_core = at(zl, y, x, zh, 1 - core)
    d_xp, d_xm = at(zl, y, xp, zh, core), at(zl, y, xm, zh, core)
    d_yp, d_ym = at(zl, yp, x, zh, core), at(zl, ym, x, zh, core)
    d_zl = at(1 - zl, y, x, zh, core)
    d_zh = at(zl, y, x, 1 - zh, core)
    lin = row * 16 + col
    has_l, has_r = lin > 0, lin < 127
    left, right = jnp.maximum(lin - 1, 0), jnp.minimum(lin + 1, 127)
    d_left, d_right = (left // 16, left % 16), (right // 16, right % 16)

    own = pl.ds(HALF * LEAF, K * LEAF)
    c_panel = pltpu.make_async_copy(panel_hbm, pext.at[own], lsem.at[0])
    c_vt = pltpu.make_async_copy(vt_hbm, vt, lsem.at[1])
    c_ct = pltpu.make_async_copy(ct_hbm, ct, lsem.at[2])
    c_ut = pltpu.make_async_copy(
        ut_hbm.at[:, pl.ds(pl.multiple_of(col * (K * LEAF), K * LEAF), K * LEAF)], ut, lsem.at[3]
    )
    c_vt.start()
    c_panel.start()

    barrier = pltpu.get_barrier_semaphore()
    for dev in (d_core, d_xp, d_xm, d_yp, d_ym, d_zl, d_zh):
        pl.semaphore_signal(barrier, inc=1, device_id=dev, device_id_type=MESH)

    @pl.when(has_l)
    def _():
        pl.semaphore_signal(barrier, inc=1, device_id=d_left, device_id_type=MESH)

    @pl.when(has_r)
    def _():
        pl.semaphore_signal(barrier, inc=1, device_id=d_right, device_id_type=MESH)

    c_ct.start()
    c_ut.start()

    def near_copy(k):
        return pltpu.make_async_copy(near_hbm.at[k], nb.at[k], nsem.at[k])

    for k in list(range(4, 12)) + list(range(0, 4)) + list(range(12, 16)):
        near_copy(k).start()

    c_vt.wait()
    c_panel.wait()
    for k in range(K):
        v = mm(
            vt[:, k * LEAF:(k + 1) * LEAF], pext[(HALF + k) * LEAF:(HALF + k + 1) * LEAF, :]
        ).astype(BF16)
        call0[row * K + k] = v[:, :HN]
        call1[row * K + k] = v[:, HN:]

    pl.semaphore_wait(barrier, 7 + has_l.astype(jnp.int32) + has_r.astype(jnp.int32))

    def rc(m, src, dst, dev):
        return pltpu.make_async_remote_copy(
            src_ref=src, dst_ref=dst, send_sem=ssem.at[m], recv_sem=rsem.at[m],
            device_id=dev, device_id_type=MESH,
        )

    call = (call0, call1)

    def piece(q, m, slot, half, dev):
        ref = call[q].at[pl.ds(slot * K + half * 8, 8)]
        return rc(14 * q + m, ref, ref, dev)

    s_zp = (1 - zl) * 4 + y
    s_ym, s_yp = zl * 4 + ym, zl * 4 + yp
    sz_ym, sz_yp = (1 - zl) * 4 + ym, (1 - zl) * 4 + yp
    ga = [[
        piece(q, 0, row, 0, d_zl), piece(q, 1, row, 1, d_zl),
        piece(q, 2, row, 0, d_yp), piece(q, 3, row, 1, d_yp),
        piece(q, 4, row, 0, d_ym), piece(q, 5, row, 1, d_ym),
        piece(q, 6, s_zp, 0, d_yp), piece(q, 7, s_zp, 1, d_yp),
        piece(q, 8, s_zp, 0, d_ym), piece(q, 9, s_zp, 1, d_ym),
        piece(q, 10, s_ym, 0, d_yp), piece(q, 11, s_yp, 1, d_ym),
        piece(q, 12, sz_ym, 0, d_yp), piece(q, 13, sz_yp, 1, d_ym),
    ] for q in range(2)]

    def relay_own(q):
        ga[q][2].wait_recv()
        ga[q][10].start()
        ga[q][5].wait_recv()
        ga[q][11].start()

    def relay_z(q):
        ga[q][0].wait_recv()
        ga[q][6].start()
        ga[q][8].start()
        ga[q][1].wait_recv()
        ga[q][9].start()
        ga[q][7].start()

    def relay_far(q):
        ga[q][6].wait_recv()
        ga[q][12].start()
        ga[q][9].wait_recv()
        ga[q][13].start()

    def gathered(q):
        for m in (3, 4, 10, 11, 7, 8, 12, 13):
            ga[q][m].wait_recv()

    for m in (0, 2, 5, 1, 3, 4):
        ga[0][m].start()
    for m in (0, 1, 2, 5):
        ga[1][m].start()

    tail = pl.ds(K * LEAF, HALF * LEAF)
    head = pl.ds(HALF * LEAF, HALF * LEAF)
    lo = pl.ds(0, HALF * LEAF)
    hi = pl.ds((HALF + K) * LEAF, HALF * LEAF)
    h_right = rc(44, pext.at[tail], pext.at[lo], d_right)
    h_left = rc(45, pext.at[head], pext.at[hi], d_left)

    expand[...] = jnp.where(
        iota((R, 256), 1) % 16 == iota((R, 256), 0), 1.0, 0.0
    ).astype(BF16)
    c_ct.wait()
    keep = iota((SLOTS, 256), 0) % 16 == iota((SLOTS, 256), 1) // 16

    def l_rows(start, stop):
        def body(b, carry):
            for u in range(4):
                i = b * 4 + u
                v = mm_t(ct[i], expand[...])
                lmat[:, i] = jnp.where(keep, v, 0.0).astype(BF16).reshape(GROUPS, 16, 256)
            return carry
        lax.fori_loop(start // 4, stop // 4, body, 0)

    l_rows(0, 8)
    relay_own(0)
    relay_z(0)
    ga[1][3].start()
    ga[1][4].start()

    @pl.when(has_r)
    def _():
        h_right.start()

    @pl.when(has_l)
    def _():
        h_left.start()

    l_rows(8, 16)

    ra = iota((ROWCL, SLOTS), 0)
    kk, dz, pos, dc = ra % 16, 1 - (ra // 16) % 2, (ra // 32) % 4, 1 - ra // 128
    dx = jnp.where(pos == 0, 2, jnp.where(pos == 1, 1, jnp.where(pos == 2, 3, 0)))
    cluster = (((x + dx) % 4) * 4 + ((zh + dz) % 2) * 2 + (core + dc) % 2) * 16 + kk
    live = iota((ROWCL, SLOTS), 1) < cnt_ref[...]
    ohr[...] = jnp.where((cluster == rows_ref[...]) & live, 1.0, 0.0).astype(BF16)

    relay_own(1)
    relay_z(1)
    relay_far(0)

    def near_row(k):
        acc = mm(nb[k, 0], pext[pl.ds(pl.multiple_of(k * LEAF, LEAF), LEAF), :])
        for o in range(1, NEAR):
            acc += mm(nb[k, o], pext[pl.ds(pl.multiple_of((k + o) * LEAF, LEAF), LEAF), :])
        nearv[k] = acc

    def near_rows(start, stop):
        def body(k, carry):
            near_copy(k).wait()
            near_row(k)
            return carry
        lax.fori_loop(start, stop, body, 0)

    near_rows(4, 6)

    def couple(q):
        def body(b, carry):
            for u in range(4):
                g = b * 4 + u
                xs = [call[q][cols_ref[0, g * 16 + s]] for s in range(16)]
                t = mm(lmat[g].reshape(256, 256), jnp.concatenate(xs, axis=0))
                t = t.astype(BF16).reshape(8, 2, 16, HN)
                rows = pl.ds(pl.multiple_of(g * 16, 16), 16)
                tmat[:, rows, :HN] = t[:, 0]
                tmat[:, rows, HN:] = t[:, 1]
            return carry
        lax.fori_loop(0, GROUPS // 4, body, 0)

    def segment_sum(q):
        def body(b, carry):
            for u in range(4):
                i = b * 4 + u
                p = mm(ohr[...], tmat[i])
                for v in range(2):
                    lanes = slice(v * HN, (v + 1) * HN)
                    pp[q, :, :, 2 * i + v] = p[:128, lanes].astype(BF16).reshape(4, 2, 16, HN)
                    po[q, :, :, 2 * i + v] = p[128:, lanes].reshape(4, 2, 16, HN)
            return carry
        lax.fori_loop(0, 2, body, 0)

    def rcb(t, q, src, dst, dev):
        return rc(28 + 2 * t + q, src, dst, dev)

    qr = range(2)
    b0 = [rcb(0, q, pp.at[q], r0.at[q], d_core) for q in qr]
    b1p = [rcb(1, q, qs.at[q, 0, 0], r1.at[q, 0], d_xp) for q in qr]
    b1m = [rcb(2, q, qs.at[q, 0, 1], r1.at[q, 1], d_xm) for q in qr]
    b2p0 = [rcb(3, q, qs.at[q, 1, 1], r2.at[q, 0, 1], d_xp) for q in qr]
    b2m1 = [rcb(4, q, qs.at[q, 2, 0], r2.at[q, 1, 0], d_xm) for q in qr]
    b2p1 = [rcb(5, q, qs.at[q, 1, 0], r2.at[q, 0, 0], d_xp) for q in qr]
    b2m0 = [rcb(6, q, qs.at[q, 2, 1], r2.at[q, 1, 1], d_xm) for q in qr]
    bz = [rcb(7, q, zs.at[q], r3.at[q], d_zh) for q in qr]

    def fold(q, pos, dzi):
        return po[q, pos, dzi] + r0[q, pos, dzi].astype(F32)

    def x_first(q):
        b0[q].wait_recv()
        qs[q, 0, 0] = fold(q, 0, 0).astype(BF16)
        qs[q, 0, 1] = fold(q, 0, 1).astype(BF16)
        b1p[q].start()
        b1m[q].start()
        qs[q, 1, 1] = fold(q, 1, 1).astype(BF16)
        qs[q, 2, 0] = fold(q, 2, 0).astype(BF16)
        b2p0[q].start()
        b2m1[q].start()

    def x_second(q):
        b1p[q].wait_recv()
        qs[q, 1, 0] = (fold(q, 1, 0) + r1[q, 0].astype(F32)).astype(BF16)
        b2p1[q].start()
        b1m[q].wait_recv()
        qs[q, 2, 1] = (fold(q, 2, 1) + r1[q, 1].astype(F32)).astype(BF16)
        b2m0[q].start()

    def z_step(q):
        b2p1[q].wait_recv()
        b2m1[q].wait_recv()
        zs[q] = (
            fold(q, 3, 0) + r2[q, 0, 0].astype(F32) + r2[q, 1, 0].astype(F32)
        ).astype(BF16)
        bz[q].start()
        b2p0[q].wait_recv()
        b2m0[q].wait_recv()
        po[q, 3, 1] = fold(q, 3, 1) + r2[q, 0, 1].astype(F32) + r2[q, 1, 1].astype(F32)

    def finish(q):
        bz[q].wait_recv()
        c = (po[q, 3, 1] + r3[q].astype(F32)).astype(BF16).reshape(256, HN)
        cplk[:, q * HN:(q + 1) * HN] = mm(perm[...], c).astype(BF16)

    gathered(0)
    couple(0)
    relay_far(1)
    segment_sum(0)
    b0[0].start()
    near_rows(6, 8)
    x_first(0)
    gathered(1)
    couple(1)
    x_second(0)
    segment_sum(1)
    b0[1].start()

    perm[...] = jnp.where(
        (iota((256, 256), 1) // 16 == iota((256, 256), 0) % 16)
        & (iota((256, 256), 1) % 16 == iota((256, 256), 0) // 16), 1.0, 0.0
    ).astype(BF16)
    near_rows(8, 10)
    x_first(1)
    z_step(0)
    near_rows(10, 12)

    @pl.when(has_l)
    def _():
        h_right.wait_recv()

    @pl.when(jnp.logical_not(has_l))
    def _():
        pext[lo] = jnp.zeros((HALF * LEAF, N), BF16)

    @pl.when(has_r)
    def _():
        h_left.wait_recv()

    @pl.when(jnp.logical_not(has_r))
    def _():
        pext[hi] = jnp.zeros((HALF * LEAF, N), BF16)

    near_rows(0, 2)
    x_second(1)
    finish(0)
    c_ut.wait()
    utt[...] = ut[...].T
    near_rows(2, 4)
    near_rows(12, 14)
    z_step(1)
    near_rows(14, 16)
    finish(1)

    def o_body(b, carry):
        for u in range(4):
            k = b * 4 + u
            far = mm(
                utt[pl.ds(pl.multiple_of(k * LEAF, LEAF), LEAF), :],
                cplk[pl.ds(pl.multiple_of(k * R, R), R), :],
            )
            rows = pl.ds(pl.multiple_of(k * LEAF, LEAF), LEAF)
            out_ref[rows, :] = (nearv[k] + far).astype(BF16)
        return carry

    lax.fori_loop(0, K // 4, o_body, 0)

    for q in qr:
        for copy in ga[q]:
            copy.wait_send()
    for group in (b0, b1p, b1m, b2p0, b2m1, b2p1, b2m0, bz):
        for copy in group:
            copy.wait_send()

    @pl.when(has_r)
    def _():
        h_right.wait_send()

    @pl.when(has_l)
    def _():
        h_left.wait_send()


def hbm(v):
    return pltpu.with_memory_space_constraint(v, pltpu.HBM)


def on_device(panel, row_basis, col_basis, near_blocks, couplings, blk_rows, blk_cols, blk_count):
    any_ = pl.BlockSpec(memory_space=pltpu.HBM)
    vm = pl.BlockSpec(memory_space=pltpu.VMEM)
    sm = pl.BlockSpec(memory_space=pltpu.SMEM)
    scratch = [
        pltpu.VMEM(((K + 2 * HALF) * LEAF, N), BF16),
        pltpu.VMEM((R, K * LEAF), BF16),
        pltpu.VMEM((R, K * LEAF), BF16),
        pltpu.VMEM((K * LEAF, R), BF16),
        pltpu.VMEM((R, R, SLOTS), BF16),
        pltpu.VMEM((K, NEAR, LEAF, LEAF), BF16),
        pltpu.VMEM((128, R, HN), BF16),
        pltpu.VMEM((128, R, HN), BF16),
        pltpu.VMEM((R, 256), BF16),
        pltpu.VMEM((256, 256), BF16),
        pltpu.VMEM((GROUPS, R, 16, 256), BF16),
        pltpu.VMEM((R // 2, SLOTS, N), BF16),
        pltpu.VMEM((ROWCL, SLOTS), BF16),
        pltpu.VMEM((2, 4, 2, R, K, HN), BF16),
        pltpu.VMEM((2, 4, 2, R, K, HN), F32),
        pltpu.VMEM((2, 4, 2, R, K, HN), BF16),
        pltpu.VMEM((2, 3, 2, R, K, HN), BF16),
        pltpu.VMEM((2, 2, R, K, HN), BF16),
        pltpu.VMEM((2, 2, 2, R, K, HN), BF16),
        pltpu.VMEM((2, R, K, HN), BF16),
        pltpu.VMEM((2, R, K, HN), BF16),
        pltpu.VMEM((K * R, N), BF16),
        pltpu.VMEM((K, LEAF, N), F32),
        pltpu.SemaphoreType.DMA((4,)),
        pltpu.SemaphoreType.DMA((K,)),
        pltpu.SemaphoreType.DMA((46,)),
        pltpu.SemaphoreType.DMA((46,)),
    ]
    return pl.pallas_call(
        kernel,
        out_shape=pltpu.VMEM((K * LEAF, N), BF16),
        in_specs=[any_, any_, any_, any_, any_, vm, sm, vm],
        out_specs=vm,
        scratch_shapes=scratch,
        compiler_params=pltpu.CompilerParams(
            collective_id=0, has_side_effects=True, vmem_limit_bytes=64_800_000
        ),
    )(
        hbm(panel),
        hbm(row_basis.T),
        hbm(col_basis.T),
        hbm(near_blocks),
        hbm(couplings.reshape(SLOTS, R, R).transpose(1, 2, 0)),
        blk_rows.reshape(1, SLOTS),
        blk_cols.reshape(1, SLOTS),
        blk_count,
    )


def solution(mesh):
    placed = (
        P(("row", "col"), None),
        P("row", None),
        P(("row", "col"), None),
        P(("row", "col"), None, None, None),
        P("row", "col", None, None, None),
        P("row", "col", None),
        P("row", "col", None),
        P("row", "col"),
    )
    return jax.shard_map(
        on_device, mesh=mesh, in_specs=placed, out_specs=P(("row", "col"), None), check_vma=False
    )
```

time: 64.6 us -> 53.1 us (0.82)
  Pallas kernels: 60.7 us -> 50.9 us
  local copies, waits for them, and re-layouts: 3.05 us -> 1.32 us
    pallas_call x1, Pallas kernels: 60.7 us -> 50.9 us  [on_device(): pl.pallas_call(kernel, out_shape=pltpu.VMEM((K * LEAF, N), BF16), in_spec...]
    unnamed x1, local copies, waits for them, and re-layouts: 3.05 us -> 1.32 us
where the time goes in v2:
time: 53.1 us; the launch traced here: 52.8 us
  Pallas kernels  50.9 us (96%)
  local copies, waits for them, and re-layouts  1.32 us (2%)
  between operations  0.66 us (1%)
    pallas_call x1, Pallas kernels, on_device(): pl.pallas_call(kernel, out_shape=pltpu.VMEM((K * LEAF, N), BF16), in_spec...  50.9 us
    unnamed x1, local copies, waits for them, and re-layouts  1.32 us

profile of v2, /device:TPU:0, one launch (start us, length us, event | category | flops | bytes accessed | tf_op | source)
XLA Modules:
  0.0 52.8 jit_solution(3418260482533713333)
XLA Ops:
  0.7 50.9 %shard_map.82 = bf16[4096,256]{1,0:T(8,128)(2,1)S(1)} custom-call(bf16[4096,256]{1,0:T(8,128)(2,1)} %panel_hbm.1, bf16[16,65536]{1,0:T(8,128)(2,1)} %bitcast.7, bf16[16,4096]{1,0:T(8,128)(2,1)} %bitcast.9, bf16[16,9,256,256]{3,2,1,0:T(8,128)(2,1)} %near_hbm.1, bf16[16,16,512]{2,1,0:T(8,128)(2,1)} %bitcast.8, s32[1,512]{1,0:T(1,128)} %bitcast.10, ...), custom_call_target="tpu_custom_call" | custom-call | tf_op jit(solution)/shard_map/pallas_call | solution.py:414
  51.5 1.3 %copy.10 = bf16[4096,256]{1,0:T(8,128)(2,1)} copy(bf16[4096,256]{1,0:T(8,128)(2,1)S(1)} %shard_map.82) | data formatting | bytes 4194304

commit v3 on v2

--- a/solution.py
+++ b/solution.py
@@ -34,10 +34,10 @@
 
 
 def kernel(
-    panel_hbm, ut_hbm, vt_hbm, near_hbm, ct_hbm, rows_ref, cols_ref, cnt_ref,
+    panel_hbm, ut_hbm, vt_hbm, near_hbm, ct_hbm, rows_hbm, cols_hbm, cnt_ref,
     out_ref,
     pext, vt, ut, utt, ct, nb, call0, call1, expand, perm, lmat, tmat, ohr,
-    pp, po, r0, qs, r1, r2, zs, r3, cplk, nearv,
+    pp, po, r0, qs, r1, r2, zs, r3, cplk, nearv, rows_ref, cols_ref,
     lsem, nsem, ssem, rsem,
 ):
     row = lax.axis_index("row")
@@ -69,6 +69,8 @@
     )
     c_vt.start()
     c_panel.start()
+    c_rows = pltpu.make_async_copy(rows_hbm, rows_ref, lsem.at[4])
+    c_cols = pltpu.make_async_copy(cols_hbm, cols_ref, lsem.at[5])
 
     barrier = pltpu.get_barrier_semaphore()
     for dev in (d_core, d_xp, d_xm, d_yp, d_ym, d_zl, d_zh):
@@ -83,13 +85,12 @@
         pl.semaphore_signal(barrier, inc=1, device_id=d_right, device_id_type=MESH)
 
     c_ct.start()
+    c_rows.start()
+    c_cols.start()
     c_ut.start()
 
     def near_copy(k):
         return pltpu.make_async_copy(near_hbm.at[k], nb.at[k], nsem.at[k])
-
-    for k in list(range(4, 12)) + list(range(0, 4)) + list(range(12, 16)):
-        near_copy(k).start()
 
     c_vt.wait()
     c_panel.wait()
@@ -167,6 +168,10 @@
         iota((R, 256), 1) % 16 == iota((R, 256), 0), 1.0, 0.0
     ).astype(BF16)
     c_ct.wait()
+    c_rows.wait()
+    c_cols.wait()
+    for k in list(range(4, 12)) + list(range(0, 4)) + list(range(12, 16)):
+        near_copy(k).start()
     keep = iota((SLOTS, 256), 0) % 16 == iota((SLOTS, 256), 1) // 16
 
     def l_rows(start, stop):
@@ -179,26 +184,19 @@
         lax.fori_loop(start // 4, stop // 4, body, 0)
 
     l_rows(0, 8)
+
     relay_own(0)
     relay_z(0)
     ga[1][3].start()
     ga[1][4].start()
 
-    @pl.when(has_r)
-    def _():
-        h_right.start()
-
-    @pl.when(has_l)
-    def _():
-        h_left.start()
-
     l_rows(8, 16)
 
     ra = iota((ROWCL, SLOTS), 0)
     kk, dz, pos, dc = ra % 16, 1 - (ra // 16) % 2, (ra // 32) % 4, 1 - ra // 128
     dx = jnp.where(pos == 0, 2, jnp.where(pos == 1, 1, jnp.where(pos == 2, 3, 0)))
     cluster = (((x + dx) % 4) * 4 + ((zh + dz) % 2) * 2 + (core + dc) % 2) * 16 + kk
-    live = iota((ROWCL, SLOTS), 1) < cnt_ref[...]
+    live = iota((ROWCL, SLOTS), 1) < cnt_ref[0, 0]
     ohr[...] = jnp.where((cluster == rows_ref[...]) & live, 1.0, 0.0).astype(BF16)
 
     relay_own(1)
@@ -220,7 +218,7 @@
 
     near_rows(4, 6)
 
-    def couple(q):
+    def couple(q, start, stop):
         def body(b, carry):
             for u in range(4):
                 g = b * 4 + u
@@ -231,7 +229,7 @@
                 tmat[:, rows, :HN] = t[:, 0]
                 tmat[:, rows, HN:] = t[:, 1]
             return carry
-        lax.fori_loop(0, GROUPS // 4, body, 0)
+        lax.fori_loop(start // 4, stop // 4, body, 0)
 
     def segment_sum(q):
         def body(b, carry):
@@ -297,15 +295,23 @@
         cplk[:, q * HN:(q + 1) * HN] = mm(perm[...], c).astype(BF16)
 
     gathered(0)
-    couple(0)
     relay_far(1)
+
+    @pl.when(has_r)
+    def _():
+        h_right.start()
+
+    @pl.when(has_l)
+    def _():
+        h_left.start()
+
+    couple(0, 0, GROUPS)
     segment_sum(0)
     b0[0].start()
-    near_rows(6, 8)
+    gathered(1)
+    couple(1, 0, GROUPS // 2)
     x_first(0)
-    gathered(1)
-    couple(1)
-    x_second(0)
+    couple(1, GROUPS // 2, GROUPS)
     segment_sum(1)
     b0[1].start()
 
@@ -313,10 +319,11 @@
         (iota((256, 256), 1) // 16 == iota((256, 256), 0) % 16)
         & (iota((256, 256), 1) % 16 == iota((256, 256), 0) // 16), 1.0, 0.0
     ).astype(BF16)
-    near_rows(8, 10)
+    near_rows(6, 7)
+    x_second(0)
     x_first(1)
+    near_rows(7, 12)
     z_step(0)
-    near_rows(10, 12)
 
     @pl.when(has_l)
     def _():
@@ -334,13 +341,12 @@
     def _():
         pext[hi] = jnp.zeros((HALF * LEAF, N), BF16)
 
-    near_rows(0, 2)
     x_second(1)
-    finish(0)
     c_ut.wait()
     utt[...] = ut[...].T
-    near_rows(2, 4)
+    near_rows(0, 4)
     near_rows(12, 14)
+    finish(0)
     z_step(1)
     near_rows(14, 16)
     finish(1)
@@ -381,7 +387,6 @@
 def on_device(panel, row_basis, col_basis, near_blocks, couplings, blk_rows, blk_cols, blk_count):
     any_ = pl.BlockSpec(memory_space=pltpu.HBM)
     vm = pl.BlockSpec(memory_space=pltpu.VMEM)
-    sm = pl.BlockSpec(memory_space=pltpu.SMEM)
     scratch = [
         pltpu.VMEM(((K + 2 * HALF) * LEAF, N), BF16),
         pltpu.VMEM((R, K * LEAF), BF16),
@@ -406,7 +411,9 @@
         pltpu.VMEM((2, R, K, HN), BF16),
         pltpu.VMEM((K * R, N), BF16),
         pltpu.VMEM((K, LEAF, N), F32),
-        pltpu.SemaphoreType.DMA((4,)),
+        pltpu.VMEM((1, SLOTS), jnp.int32),
+        pltpu.SMEM((1, SLOTS), jnp.int32),
+        pltpu.SemaphoreType.DMA((6,)),
         pltpu.SemaphoreType.DMA((K,)),
         pltpu.SemaphoreType.DMA((46,)),
         pltpu.SemaphoreType.DMA((46,)),
@@ -414,7 +421,7 @@
     return pl.pallas_call(
         kernel,
         out_shape=pltpu.VMEM((K * LEAF, N), BF16),
-        in_specs=[any_, any_, any_, any_, any_, vm, sm, vm],
+        in_specs=[any_] * 7 + [pl.BlockSpec(memory_space=pltpu.SMEM)],
         out_specs=vm,
         scratch_shapes=scratch,
         compiler_params=pltpu.CompilerParams(
@@ -426,8 +433,8 @@
         hbm(col_basis.T),
         hbm(near_blocks),
         hbm(couplings.reshape(SLOTS, R, R).transpose(1, 2, 0)),
-        blk_rows.reshape(1, SLOTS),
-        blk_cols.reshape(1, SLOTS),
+        hbm(blk_rows.reshape(1, SLOTS)),
+        hbm(blk_cols.reshape(1, SLOTS)),
         blk_count,
     )
 

time: 53.1 us -> 45.6 us (0.86)
  the two profiles are of different devices: /device:TPU:0 before, /device:TPU:8 now
where the time goes in v3:
time: 45.6 us; the launch traced here: 45.4 us
  Pallas kernels  43.5 us (95%)
  local copies, waits for them, and re-layouts  1.32 us (3%)
  between operations  0.66 us (1%)
    pallas_call x1, Pallas kernels, on_device(): pl.pallas_call(kernel, out_shape=pltpu.VMEM((K * LEAF, N), BF16), in_spec...  43.5 us
    unnamed x1, local copies, waits for them, and re-layouts  1.32 us

profile of v3, /device:TPU:8, one launch (start us, length us, event | category | flops | bytes accessed | tf_op | source)
XLA Modules:
  0.0 45.4 jit_solution(15018851484917346044)
XLA Ops:
  0.7 43.5 %shard_map.82 = bf16[4096,256]{1,0:T(8,128)(2,1)S(1)} custom-call(bf16[4096,256]{1,0:T(8,128)(2,1)} %panel_hbm.1, bf16[16,65536]{1,0:T(8,128)(2,1)} %bitcast.7, bf16[16,4096]{1,0:T(8,128)(2,1)} %bitcast.9, bf16[16,9,256,256]{3,2,1,0:T(8,128)(2,1)} %near_hbm.1, bf16[16,16,512]{2,1,0:T(8,128)(2,1)} %bitcast.8, s32[1,512]{1,0:T(1,128)} %bitcast.10, ...), custom_call_target="tpu_custom_call" | custom-call | tf_op jit(solution)/shard_map/pallas_call | solution.py:421
  44.1 1.3 %copy.10 = bf16[4096,256]{1,0:T(8,128)(2,1)} copy(bf16[4096,256]{1,0:T(8,128)(2,1)S(1)} %shard_map.82) | data formatting | bytes 4194304

commit v4 on v3

--- a/solution.py
+++ b/solution.py
@@ -54,6 +54,7 @@
     d_xp, d_xm = at(zl, y, xp, zh, core), at(zl, y, xm, zh, core)
     d_yp, d_ym = at(zl, yp, x, zh, core), at(zl, ym, x, zh, core)
     d_zl = at(1 - zl, y, x, zh, core)
+    d_y2 = at(zl, (y + 2) % 4, x, zh, core)
     d_zh = at(zl, y, x, 1 - zh, core)
     lin = row * 16 + col
     has_l, has_r = lin > 0, lin < 127
@@ -73,7 +74,7 @@
     c_cols = pltpu.make_async_copy(cols_hbm, cols_ref, lsem.at[5])
 
     barrier = pltpu.get_barrier_semaphore()
-    for dev in (d_core, d_xp, d_xm, d_yp, d_ym, d_zl, d_zh):
+    for dev in (d_core, d_xp, d_xm, d_yp, d_ym, d_y2, d_zl, d_zh):
         pl.semaphore_signal(barrier, inc=1, device_id=dev, device_id_type=MESH)
 
     @pl.when(has_l)
@@ -101,7 +102,7 @@
         call0[row * K + k] = v[:, :HN]
         call1[row * K + k] = v[:, HN:]
 
-    pl.semaphore_wait(barrier, 7 + has_l.astype(jnp.int32) + has_r.astype(jnp.int32))
+    pl.semaphore_wait(barrier, 8 + has_l.astype(jnp.int32) + has_r.astype(jnp.int32))
 
     def rc(m, src, dst, dev):
         return pltpu.make_async_remote_copy(
@@ -117,7 +118,6 @@
 
     s_zp = (1 - zl) * 4 + y
     s_ym, s_yp = zl * 4 + ym, zl * 4 + yp
-    sz_ym, sz_yp = (1 - zl) * 4 + ym, (1 - zl) * 4 + yp
     ga = [[
         piece(q, 0, row, 0, d_zl), piece(q, 1, row, 1, d_zl),
         piece(q, 2, row, 0, d_yp), piece(q, 3, row, 1, d_yp),
@@ -125,7 +125,7 @@
         piece(q, 6, s_zp, 0, d_yp), piece(q, 7, s_zp, 1, d_yp),
         piece(q, 8, s_zp, 0, d_ym), piece(q, 9, s_zp, 1, d_ym),
         piece(q, 10, s_ym, 0, d_yp), piece(q, 11, s_yp, 1, d_ym),
-        piece(q, 12, sz_ym, 0, d_yp), piece(q, 13, sz_yp, 1, d_ym),
+        piece(q, 12, s_zp, 0, d_y2), piece(q, 13, s_zp, 1, d_y2),
     ] for q in range(2)]
 
     def relay_own(q):
@@ -136,25 +136,21 @@
 
     def relay_z(q):
         ga[q][0].wait_recv()
+        ga[q][12].start()
         ga[q][6].start()
         ga[q][8].start()
         ga[q][1].wait_recv()
+        ga[q][13].start()
         ga[q][9].start()
         ga[q][7].start()
 
-    def relay_far(q):
-        ga[q][6].wait_recv()
-        ga[q][12].start()
-        ga[q][9].wait_recv()
-        ga[q][13].start()
-
     def gathered(q):
-        for m in (3, 4, 10, 11, 7, 8, 12, 13):
+        for m in (3, 4, 10, 11, 6, 9, 7, 8, 12, 13):
             ga[q][m].wait_recv()
 
     for m in (0, 2, 5, 1, 3, 4):
         ga[0][m].start()
-    for m in (0, 1, 2, 5):
+    for m in (0, 1, 2, 5, 3, 4):
         ga[1][m].start()
 
     tail = pl.ds(K * LEAF, HALF * LEAF)
@@ -187,8 +183,6 @@
 
     relay_own(0)
     relay_z(0)
-    ga[1][3].start()
-    ga[1][4].start()
 
     l_rows(8, 16)
 
@@ -201,7 +195,6 @@
 
     relay_own(1)
     relay_z(1)
-    relay_far(0)
 
     def near_row(k):
         acc = mm(nb[k, 0], pext[pl.ds(pl.multiple_of(k * LEAF, LEAF), LEAF), :])
@@ -247,7 +240,12 @@
         return rc(28 + 2 * t + q, src, dst, dev)
 
     qr = range(2)
-    b0 = [rcb(0, q, pp.at[q], r0.at[q], d_core) for q in qr]
+    b0 = [[rc(46 + 4 * q + p, pp.at[q, p], r0.at[q, p], d_core) for p in range(4)] for q in qr]
+
+    def core_send(q):
+        for copy in b0[q]:
+            copy.start()
+
     b1p = [rcb(1, q, qs.at[q, 0, 0], r1.at[q, 0], d_xp) for q in qr]
     b1m = [rcb(2, q, qs.at[q, 0, 1], r1.at[q, 1], d_xm) for q in qr]
     b2p0 = [rcb(3, q, qs.at[q, 1, 1], r2.at[q, 0, 1], d_xp) for q in qr]
@@ -260,11 +258,13 @@
         return po[q, pos, dzi] + r0[q, pos, dzi].astype(F32)
 
     def x_first(q):
-        b0[q].wait_recv()
+        b0[q][0].wait_recv()
         qs[q, 0, 0] = fold(q, 0, 0).astype(BF16)
         qs[q, 0, 1] = fold(q, 0, 1).astype(BF16)
         b1p[q].start()
         b1m[q].start()
+        b0[q][1].wait_recv()
+        b0[q][2].wait_recv()
         qs[q, 1, 1] = fold(q, 1, 1).astype(BF16)
         qs[q, 2, 0] = fold(q, 2, 0).astype(BF16)
         b2p0[q].start()
@@ -279,6 +279,7 @@
         b2m0[q].start()
 
     def z_step(q):
+        b0[q][3].wait_recv()
         b2p1[q].wait_recv()
         b2m1[q].wait_recv()
         zs[q] = (
@@ -295,7 +296,6 @@
         cplk[:, q * HN:(q + 1) * HN] = mm(perm[...], c).astype(BF16)
 
     gathered(0)
-    relay_far(1)
 
     @pl.when(has_r)
     def _():
@@ -307,13 +307,13 @@
 
     couple(0, 0, GROUPS)
     segment_sum(0)
-    b0[0].start()
+    core_send(0)
     gathered(1)
     couple(1, 0, GROUPS // 2)
     x_first(0)
     couple(1, GROUPS // 2, GROUPS)
     segment_sum(1)
-    b0[1].start()
+    core_send(1)
 
     perm[...] = jnp.where(
         (iota((256, 256), 1) // 16 == iota((256, 256), 0) % 16)
@@ -367,7 +367,7 @@
     for q in qr:
         for copy in ga[q]:
             copy.wait_send()
-    for group in (b0, b1p, b1m, b2p0, b2m1, b2p1, b2m0, bz):
+    for group in (b0[0], b0[1], b1p, b1m, b2p0, b2m1, b2p1, b2m0, bz):
         for copy in group:
             copy.wait_send()
 
@@ -415,8 +415,8 @@
         pltpu.SMEM((1, SLOTS), jnp.int32),
         pltpu.SemaphoreType.DMA((6,)),
         pltpu.SemaphoreType.DMA((K,)),
-        pltpu.SemaphoreType.DMA((46,)),
-        pltpu.SemaphoreType.DMA((46,)),
+        pltpu.SemaphoreType.DMA((54,)),
+        pltpu.SemaphoreType.DMA((54,)),
     ]
     return pl.pallas_call(
         kernel,

time: 45.6 us -> 45.2 us (level)
  the two profiles are of different devices: /device:TPU:8 before, /device:TPU:0 now
where the time goes in v4:
time: 45.2 us; the launch traced here: 45.1 us
  Pallas kernels  43.1 us (95%)
  local copies, waits for them, and re-layouts  1.32 us (3%)
  between operations  0.66 us (1%)
    pallas_call x1, Pallas kernels, on_device(): pl.pallas_call(kernel, out_shape=pltpu.VMEM((K * LEAF, N), BF16), in_spec...  43.1 us
    unnamed x1, local copies, waits for them, and re-layouts  1.32 us

profile of v4, /device:TPU:0, one launch (start us, length us, event | category | flops | bytes accessed | tf_op | source)
XLA Modules:
  0.0 45.1 jit_solution(97849986546626714)
XLA Ops:
  0.7 43.1 %shard_map.82 = bf16[4096,256]{1,0:T(8,128)(2,1)S(1)} custom-call(bf16[4096,256]{1,0:T(8,128)(2,1)} %panel_hbm.1, bf16[16,65536]{1,0:T(8,128)(2,1)} %bitcast.7, bf16[16,4096]{1,0:T(8,128)(2,1)} %bitcast.9, bf16[16,9,256,256]{3,2,1,0:T(8,128)(2,1)} %near_hbm.1, bf16[16,16,512]{2,1,0:T(8,128)(2,1)} %bitcast.8, s32[1,512]{1,0:T(1,128)} %bitcast.10, ...), custom_call_target="tpu_custom_call" | custom-call | tf_op jit(solution)/shard_map/pallas_call | solution.py:421
  43.8 1.3 %copy.10 = bf16[4096,256]{1,0:T(8,128)(2,1)} copy(bf16[4096,256]{1,0:T(8,128)(2,1)S(1)} %shard_map.82) | data formatting | bytes 4194304
